TPU v7x, 128 devices: a whole 4x4x4 slice. The times are simulated.
128 devices in a mesh: gx: 8 (over x, core), gy: 16 (over y, z).
Axes of the slice: x: 4, y: 4, z: 4, core: 2. Of those that a mesh axis runs over, the one named last changes fastest.
Arguments:
- tokens: bfloat16 [512, 8192], P('gy', 'gx'), may hold values from -6 to 6
- up_old: bfloat16 [32768, 8192], P(('gx', 'gy')), may hold values from -0.0625 to 0.0625
- down_old: bfloat16 [32768, 8192], P(('gx', 'gy')), may hold values from -0.0625 to 0.0625
- old_slot: int32 [256], replicated, may hold values from 0 to 255, as said below
- new_owner: int32 [256], replicated, may hold values from 0 to 127, as said below
- hot_rank: int32 [256], replicated, may hold values from 0 to 1, as said below
- route: int32 [512], replicated, may hold values from 0 to 511, each once
Outputs:
- up_new: bfloat16 [32768, 8192], P(('gx', 'gy'))
- down_new: bfloat16 [32768, 8192], P(('gx', 'gy'))
- mixed: bfloat16 [512, 8192], P('gy', 'gx')
Inputs may be any that keep to these rules, and one draw needn't show every extreme that they name: `old_slot`: each slot number appears exactly once. `new_owner`: each device index is the new owner of exactly 2 blocks. `hot_rank`: the blocks of one new owner have distinct ranks.
All inputs are finite; a program needn't handle non-finite values.
Results may differ from a plain program's by a relative error of at most 0.0049.
Values may be sent and summed in bfloat16 or wider, within the bound.
A program may use at most 128 MiB of HBM per device.

v0:
```python
import jax
import jax.numpy as jnp
from jax import lax
from jax.sharding import PartitionSpec as P

BLOCK = 128


def split_up(shard, dim, peers):
    lengths = shard.shape
    parts = shard.reshape(*lengths[:dim], peers, lengths[dim] // peers, *lengths[dim + 1 :])
    return jnp.moveaxis(parts, dim, 0)


def laid_out(parts, dim):
    parts = jnp.moveaxis(parts, 0, dim)
    lengths = parts.shape
    return parts.reshape(*lengths[:dim], lengths[dim] * lengths[dim + 1], *lengths[dim + 2 :])


def exchange_both(shard, axis, axes, splits, concats):
    sizes = [lax.axis_size(a) for a in axes]
    parts = split_up(shard, splits[0], sizes[0])
    parts = jnp.moveaxis(split_up(parts, splits[1] + 1, sizes[1]), 0, 1)
    inside = parts.shape[2:]
    parts = parts.reshape(-1, *inside)
    parts = lax.all_to_all(parts, axis, split_axis=0, concat_axis=0, tiled=True)
    parts = laid_out(parts.reshape(*sizes, *inside), concats[0] + 1)
    return laid_out(parts, concats[1])


def sum_at_owner(shard, axis, dim):
    parts = split_up(shard, dim, lax.axis_size(axis))
    arrived = lax.all_to_all(parts, axis, split_axis=0, concat_axis=0, tiled=True)
    return arrived.sum(axis=0)


def layer_terms(ordered, up_rows, down_rows):
    pre = lax.dot_general(
        ordered, up_rows, (((1,), (1,)), ((), ())), preferred_element_type=jnp.float32
    )
    hidden = jax.nn.gelu(pre, approximate=False).astype(jnp.bfloat16)
    return jnp.dot(hidden, down_rows, preferred_element_type=jnp.float32)


def relocate(up_old, down_old, old_slot, new_owner, hot_rank):
    held = up_old.shape[0] // BLOCK
    width = up_old.shape[1]
    shaped = (up_old.reshape(held, BLOCK, width), down_old.reshape(held, BLOCK, width))
    across_x = lax.axis_size("gx")
    across_y = lax.axis_size("gy")
    sectioned = (
        exchange_both(shaped[0], ("gx", "gy"), ("gx", "gy"), (1, 1), (0, 0)),
        exchange_both(shaped[1], ("gx", "gy"), ("gx", "gy"), (1, 1), (0, 0)),
    )
    share = sectioned[0].shape[1]

    def reorder(arr):
        arr = arr.reshape(across_y, across_x, held, share, width)
        return jnp.transpose(arr, (1, 0, 2, 3, 4)).reshape(across_x * across_y * held, share, width)

    spread = (reorder(sectioned[0]), reorder(sectioned[1]))
    total = spread[0].shape[0]
    new_slot = new_owner * held + hot_rank
    source = jnp.zeros((total,), jnp.int32).at[new_slot].set(old_slot)
    picked = (jnp.take(spread[0], source, axis=0), jnp.take(spread[1], source, axis=0))
    landed = (
        lax.all_to_all(picked[0], ("gx", "gy"), split_axis=0, concat_axis=1, tiled=True),
        lax.all_to_all(picked[1], ("gx", "gy"), split_axis=0, concat_axis=1, tiled=True),
    )
    return (landed[0].reshape(held * BLOCK, width), landed[1].reshape(held * BLOCK, width))


def shards(tokens, up_old, down_old, old_slot, new_owner, hot_rank, route):
    feature_rows = lax.all_gather(tokens, "gx", axis=1, tiled=True)
    everyone = lax.all_gather(feature_rows, "gy", axis=0, tiled=True)
    ordered = jnp.take(everyone, route, axis=0)
    up_new, down_new = relocate(up_old, down_old, old_slot, new_owner, hot_rank)
    partial_out = layer_terms(ordered, up_new, down_new)
    by_columns = lax.psum_scatter(partial_out, "gx", scatter_dimension=1, tiled=True)
    summed = sum_at_owner(by_columns, "gy", 0)
    return (up_new, down_new, summed.astype(jnp.bfloat16))


def solution(mesh):
    in_specs = (P("gy", "gx"), P(("gx", "gy"), None), P(("gx", "gy"), None), P(), P(), P(), P())
    out_specs = (P(("gx", "gy"), None), P(("gx", "gy"), None), P("gy", "gx"))
    return jax.shard_map(shards, mesh=mesh, in_specs=in_specs, out_specs=out_specs, check_vma=False)
```

profile of v0, /device:TPU:0, one launch (start us, length us, event | category | flops | bytes accessed | tf_op | source)
XLA Modules:
  0.0 561.5 jit_solution(2574933312884499092)
XLA Ops:
  7.2 8.6 %copy.24 = bf16[2,8,16,8192]{3,0,2,1:T(2,128)(2,1)} copy(bf16[2,8,16,8192]{3,2,1,0:T(8,128)(2,1)} %bitcast.36) | data formatting | bytes 8388608 | tf_op jit(solution)/shard_map/reshape;reshape | solution.py:11
  15.7 0.0 copy-start
  15.7 11.7 %all-to-all-start = ((bf16[128,2,1,8192]{3,1,2,0:T(2,128)(2,1)}), bf16[128,2,1,8192]{3,1,2,0:T(2,128)(2,1)}, u32[]{:S(2)}, u32[]{:S(2)}) async-start(bf16[128,2,1,8192]{3,1,2,0:T(2,128)(2,1)} %bitcast.33), calls=%async_computation | async-start | bytes 8388608 | tf_op jit(solution)/shard_map/all_to_all | solution.py:27
  27.5 0.0 all-gather.2.cloned.1.call-start
  27.5 0.0 copy-done
  27.5 55.9 %all_gather.6 = bf16[32,8192]{1,0:T(8,128)(2,1)} all-gather(bf16[32,1024]{1,0:T(8,128)(2,1)S(1)} %copy-done), channel_id=1, replica_groups=mesh['gx'=8,'gy'=16] {'gx'}, dimensions={1}, use_global_device_ids=true | all-gather | bytes 589824 | tf_op jit(solution)/shard_map/all_gather | solution.py:75
  83.5 0.0 all-gather.2.cloned.1.call-update
  83.5 8.6 %copy.27 = bf16[2,8,16,8192]{3,0,2,1:T(2,128)(2,1)} copy(bf16[2,8,16,8192]{3,2,1,0:T(8,128)(2,1)} %bitcast.37) | data formatting | bytes 8388608 | tf_op jit(solution)/shard_map/reshape;reshape | solution.py:11
  92.1 0.0 all-to-all-done
  92.1 0.0 copy-start.2
  92.1 0.0 copy-start.3
  92.1 10.7 %all-to-all-start.2 = ((bf16[128,2,1,8192]{3,1,2,0:T(2,128)(2,1)}), bf16[128,2,1,8192]{3,1,2,0:T(2,128)(2,1)}, u32[]{:S(2)}, u32[]{:S(2)}) async-start(bf16[128,2,1,8192]{3,1,2,0:T(2,128)(2,1)} %bitcast.32), calls=%async_computation.2 | async-start | bytes 8388608 | tf_op jit(solution)/shard_map/all_to_all | solution.py:27
  102.8 0.0 copy-done.2
  102.8 0.0 copy-done.3
  102.8 1.6 scatter_custom_fusion
  104.4 7.2 %reshape.111 = bf16[256,8192]{1,0:T(8,128)(2,1)} reshape(bf16[128,2,1,8192]{3,1,2,0:T(2,128)(2,1)} %all-to-all-done) | data formatting | bytes 8388608 | tf_op jit(solution)/shard_map/jit(_take)/Arg_0.7 | solution.py:66
  111.6 11.7 %gather_fusion.1 = bf16[256,8192]{1,0:T(8,128)(2,1)} fusion(bf16[256,8192]{1,0:T(8,128)(2,1)} %reshape.111, s32[1024]{0:T(1024)S(1)} %pad_clamp_fusion.1), kind=kCustom, calls=%fused_computation.clone | custom fusion | bytes 8389632 | tf_op jit(solution)/shard_map/jit(_take)/gather | solution.py:66
  123.3 32.9 %all-to-all-done.2 = bf16[128,2,1,8192]{3,1,2,0:T(2,128)(2,1)} async-done(((bf16[128,2,1,8192]{3,1,2,0:T(2,128)(2,1)}), bf16[128,2,1,8192]{3,1,2,0:T(2,128)(2,1)}, u32[]{:S(2)}, u32[]{:S(2)}) %all-to-all-start.2) | async-done | bytes 4194336 | tf_op jit(solution)/shard_map/all_to_all | solution.py:27
  156.3 7.7 %reshape.115 = bf16[256,8192]{1,0:T(8,128)(2,1)} reshape(bf16[128,2,1,8192]{3,1,2,0:T(2,128)(2,1)} %all-to-all-done.2) | data formatting | bytes 8388608 | tf_op jit(solution)/shard_map/jit(_take)/Arg_0.7 | solution.py:66
  164.0 11.7 %gather_fusion.2 = bf16[256,8192]{1,0:T(8,128)(2,1)} fusion(bf16[256,8192]{1,0:T(8,128)(2,1)} %reshape.115, s32[1024]{0:T(1024)S(1)} %pad_clamp_fusion.1), kind=kCustom, calls=%fused_computation.1.clone | custom fusion | bytes 8389632 | tf_op jit(solution)/shard_map/jit(_take)/gather | solution.py:66
  175.7 6.0 %bitcast_select_fusion = (bf16[256,1,8192]{2,0,1:T(8,128)(2,1)}, bf16[256,1,8192]{2,0,1:T(8,128)(2,1)}) fusion(bf16[256,8192]{1,0:T(8,128)(2,1)} %gather_fusion.2, pred[256]{0:T(512)(128)(4,1)S(1)} %compare_and_fusion, bf16[256,8192]{1,0:T(8,128)(2,1)} %gather_fusion.1), kind=kLoop, calls=%fused_computation.7 | loop fusion | flops 4194304 | bytes 16777472 | tf_op jit(solution)/shard_map/jit(_take)/select_n | solution.py:66
  181.8 0.5 broadcast.59
  182.3 6.8 %reduce.2 = bf16[256,8192]{1,0:T(8,128)(2,1)} reduce(bf16[256,1,8192]{2,0,1:T(8,128)(2,1)} %get-tuple-element.5, bf16[]{:T(256)} %broadcast.59), dimensions={1}, to_apply=%copy.25.reduce_sub_computation | reduce | bytes 8388610 | tf_op jit(solution)/shard_map/jit(_take)/select_n | solution.py:66
  189.1 7.6 %reshape.125 = bf16[128,2,8192]{2,1,0:T(2,128)(2,1)} reshape(bf16[256,8192]{1,0:T(8,128)(2,1)} %reduce.2) | data formatting | bytes 8388608
  196.7 7.7 %all-to-all-start.1 = ((bf16[128,2,8192]{2,1,0:T(2,128)(2,1)}), bf16[128,2,8192]{2,1,0:T(2,128)(2,1)}, u32[]{:S(2)}, u32[]{:S(2)}) async-start(bf16[128,2,8192]{2,1,0:T(2,128)(2,1)} %reshape.125), calls=%async_computation.1 | async-start | bytes 8388608 | tf_op jit(solution)/shard_map/all_to_all | solution.py:68
  204.5 6.7 %reduce.3 = bf16[256,8192]{1,0:T(8,128)(2,1)} reduce(bf16[256,1,8192]{2,0,1:T(8,128)(2,1)} %get-tuple-element.4, bf16[]{:T(256)} %broadcast.59), dimensions={1}, to_apply=%copy.28.reduce_sub_computation | reduce | bytes 8388610 | tf_op jit(solution)/shard_map/jit(_take)/select_n | solution.py:66
  211.2 7.6 %reshape.127 = bf16[128,2,8192]{2,1,0:T(2,128)(2,1)} reshape(bf16[256,8192]{1,0:T(8,128)(2,1)} %reduce.3) | data formatting | bytes 8388608
  218.8 0.0 copy-start.1
  218.8 38.0 %all-to-all-done.1 = bf16[128,2,8192]{2,1,0:T(2,128)(2,1)} async-done(((bf16[128,2,8192]{2,1,0:T(2,128)(2,1)}), bf16[128,2,8192]{2,1,0:T(2,128)(2,1)}, u32[]{:S(2)}, u32[]{:S(2)}) %all-to-all-start.1) | async-done | bytes 4194336 | tf_op jit(solution)/shard_map/all_to_all | solution.py:68
  256.8 5.8 %all-to-all-start.3 = ((bf16[128,2,8192]{2,1,0:T(2,128)(2,1)}), bf16[128,2,8192]{2,1,0:T(2,128)(2,1)}, u32[]{:S(2)}, u32[]{:S(2)}) async-start(bf16[128,2,8192]{2,1,0:T(2,128)(2,1)} %reshape.127), calls=%async_computation.3 | async-start | bytes 8388608 | tf_op jit(solution)/shard_map/all_to_all | solution.py:69
  262.6 0.0 reduce-scatter.2.cloned.1.call-start
  262.7 0.0 copy-done.1
  262.7 19.8 %reshape.126 = bf16[256,1,8192]{2,1,0:T(2,128)(2,1)} reshape(bf16[128,2,8192]{2,1,0:T(2,128)(2,1)} %all-to-all-done.1) | data formatting | bytes 8388608
  282.5 26.3 %reduce = bf16[256,8192]{1,0:T(8,128)(2,1)} reduce(bf16[256,1,8192]{2,1,0:T(2,128)(2,1)} %reshape.126, bf16[]{:T(256)} %constant.92), dimensions={1}, to_apply=%all_to_all.32.reduce_sub_computation | reduce | bytes 8388610 | tf_op jit(solution)/shard_map/all_to_all | solution.py:68
  308.7 7.7 %all_to_all.33 = bf16[128,2,1,8192]{3,1,0,2:T(2,128)(2,1)} reshape(bf16[256,8192]{1,0:T(8,128)(2,1)} %reduce) | data formatting | bytes 8388608 | tf_op jit(solution)/shard_map/all_to_all | solution.py:68
  316.4 6.9 %copy.26 = bf16[2,128,1,8192]{3,1,0,2:T(8,128)(2,1)} copy(bf16[2,128,1,8192]{3,0,1,2:T(2,128)(2,1)} %bitcast.34) | data formatting | bytes 8388608 | tf_op jit(solution)/shard_map/all_to_all | solution.py:68
  323.3 0.0 all-to-all-done.3
  323.3 19.8 %reshape.128 = bf16[256,1,8192]{2,1,0:T(2,128)(2,1)} reshape(bf16[128,2,8192]{2,1,0:T(2,128)(2,1)} %all-to-all-done.3) | data formatting | bytes 8388608
  343.1 26.3 %reduce.1 = bf16[256,8192]{1,0:T(8,128)(2,1)} reduce(bf16[256,1,8192]{2,1,0:T(2,128)(2,1)} %reshape.128, bf16[]{:T(256)} %constant.92), dimensions={1}, to_apply=%all_to_all.36.reduce_sub_computation | reduce | bytes 8388610 | tf_op jit(solution)/shard_map/all_to_all | solution.py:69
  369.3 7.9 %all_to_all.37 = bf16[128,2,1,8192]{3,1,0,2:T(2,128)(2,1)} reshape(bf16[256,8192]{1,0:T(8,128)(2,1)} %reduce.1) | data formatting | bytes 8388608 | tf_op jit(solution)/shard_map/all_to_all | solution.py:69
  377.2 6.9 %copy.29 = bf16[2,128,1,8192]{3,1,0,2:T(8,128)(2,1)} copy(bf16[2,128,1,8192]{3,0,1,2:T(2,128)(2,1)} %bitcast.35) | data formatting | bytes 8388608 | tf_op jit(solution)/shard_map/all_to_all | solution.py:69
  384.1 0.0 all-gather.2.cloned.1.call-done
  384.1 20.2 %gather_fusion = bf16[512,8192]{1,0:T(8,128)(2,1)} fusion(bf16[512,8192]{1,0:T(8,128)(2,1)} %all-gather.2.cloned.1.call-done, s32[1024]{0:T(1024)S(1)} %pad_clamp_fusion), kind=kCustom, calls=%fused_computation.2 | custom fusion | bytes 16779264 | tf_op jit(solution)/shard_map/jit(_take)/gather | solution.py:77
  404.3 21.5 %fusion.17 = f32[512,8192]{1,0:T(8,128)} fusion(bf16[256,8192]{1,0:T(8,128)(2,1)} %bitcast.40, bf16[256,8192]{1,0:T(8,128)(2,1)} %bitcast.38, bf16[512,8192]{1,0:T(8,128)(2,1)} %gather_fusion, pred[512]{0:T(512)(128)(4,1)S(1)} %compare_and_fusion.1), kind=kOutput, calls=%fused_computation.29 | convolution fusion | flops 4307681280 | bytes 33554944 | tf_op jit(solution)/shard_map/dot_general | solution.py:43
  425.7 0.0 reduce-scatter.2.cloned.1.call-update
  425.8 92.9 %reduce-scatter.2.cloned.1.call-done = f32[512,1024]{1,0:T(8,128)} async-done(((f32[512,8192]{1,0:T(8,128)}), f32[512,1024]{1,0:T(8,128)}) %reduce-scatter.2.cloned.1.call-update) | async-done | bytes 2097168 | tf_op jit(solution)/shard_map/reduce_scatter | solution.py:80
  518.6 34.8 %all_to_all.45 = f32[16,32,1024]{2,1,0:T(8,128)S(1)} all-to-all(f32[16,32,1024]{2,1,0:T(8,128)} %bitcast.42), channel_id=1, replica_groups=mesh['gx'=8,'gy'=16] {'gy'}, dimensions={0} | all-to-all | bytes 4194304 | tf_op jit(solution)/shard_map/all_to_all | solution.py:34
  553.5 0.7 reduce_sum.9
  (7 shorter events, 0.0 us)
Async XLA Ops:
  15.7 11.8 %copy-start = (bf16[32,1024]{1,0:T(8,128)(2,1)S(1)}, bf16[32,1024]{1,0:T(8,128)(2,1)}, u32[]{:S(2)}) copy-start(bf16[32,1024]{1,0:T(8,128)(2,1)} %param.9) | copy-start | bytes 196612
  15.7 76.3 %all-to-all-start = ((bf16[128,2,1,8192]{3,1,2,0:T(2,128)(2,1)}), bf16[128,2,1,8192]{3,1,2,0:T(2,128)(2,1)}, u32[]{:S(2)}, u32[]{:S(2)}) async-start(bf16[128,2,1,8192]{3,1,2,0:T(2,128)(2,1)} %bitcast.33), calls=%async_computation | async-start | bytes 8388608 | tf_op jit(solution)/shard_map/all_to_all | solution.py:27
  27.5 356.7 %all-gather.2.cloned.1.call-start = ((), (), s32[]{:S(2)}) async-start(), calls=%async_computation.6 | async-start | bytes 8912896 | tf_op jit(solution)/shard_map/all_gather | solution.py:76
  92.1 10.8 %copy-start.2 = (s32[256]{0:T(256)S(1)}, s32[256]{0:T(256)}, u32[]{:S(2)}) copy-start(s32[256]{0:T(256)} %param.14) | copy-start | bytes 3076
  92.1 10.8 %copy-start.3 = (s32[256]{0:T(256)S(1)}, s32[256]{0:T(256)}, u32[]{:S(2)}) copy-start(s32[256]{0:T(256)} %param.13) | copy-start | bytes 3076
  92.1 64.2 %all-to-all-start.2 = ((bf16[128,2,1,8192]{3,1,2,0:T(2,128)(2,1)}), bf16[128,2,1,8192]{3,1,2,0:T(2,128)(2,1)}, u32[]{:S(2)}, u32[]{:S(2)}) async-start(bf16[128,2,1,8192]{3,1,2,0:T(2,128)(2,1)} %bitcast.32), calls=%async_computation.2 | async-start | bytes 8388608 | tf_op jit(solution)/shard_map/all_to_all | solution.py:27
  196.7 60.0 %all-to-all-start.1 = ((bf16[128,2,8192]{2,1,0:T(2,128)(2,1)}), bf16[128,2,8192]{2,1,0:T(2,128)(2,1)}, u32[]{:S(2)}, u32[]{:S(2)}) async-start(bf16[128,2,8192]{2,1,0:T(2,128)(2,1)} %reshape.125), calls=%async_computation.1 | async-start | bytes 8388608 | tf_op jit(solution)/shard_map/all_to_all | solution.py:68
  218.8 43.8 %copy-start.1 = (s32[512]{0:T(512)S(1)}, s32[512]{0:T(512)}, u32[]{:S(2)}) copy-start(s32[512]{0:T(512)} %param.15) | copy-start | bytes 6148
  256.8 66.5 %all-to-all-start.3 = ((bf16[128,2,8192]{2,1,0:T(2,128)(2,1)}), bf16[128,2,8192]{2,1,0:T(2,128)(2,1)}, u32[]{:S(2)}, u32[]{:S(2)}) async-start(bf16[128,2,8192]{2,1,0:T(2,128)(2,1)} %reshape.127), calls=%async_computation.3 | async-start | bytes 8388608 | tf_op jit(solution)/shard_map/all_to_all | solution.py:69
  262.6 256.0 %reduce-scatter.2.cloned.1.call-start = ((), (), s32[]{:S(2)}) async-start(), calls=%async_computation.7 | async-start | bytes 18874368 | tf_op jit(solution)/shard_map/reduce_scatter | solution.py:80
Sparse Core Ops, SparseCore 0:
  83.6 115.8 all-gather.1
  425.9 92.7 reduce-scatter.1
where the time goes:
time: 572 us; the launch traced here: 561 us
  waiting for transfers between devices  164 us (29%)
  local copies, waits for them, and re-layouts  162 us (28%)
  blocking collectives  90.8 us (16%)
  other arithmetic  72.9 us (13%)
  starting transfers between devices  36.1 us (6%)
  matrix products  21.5 us (4%)
  between operations  14.6 us (3%)
    reduce_scatter x1, waiting for transfers between devices, shards(): lax.psum_scatter(partial_out, 'gx', scatter_dimension=1, tiled=True)  92.9 us
    all_gather x1, blocking collectives, shards(): feature_rows = lax.all_gather(tokens, 'gx', axis=1, tiled=True)  55.9 us
    unnamed x12, local copies, waits for them, and re-layouts  54.8 us
    all_to_all x1, waiting for transfers between devices, relocate(): lax.all_to_all(picked[0], ('gx', 'gy'), split_axis=0, concat_axis=1, tile...  38 us
    all_to_all x1, blocking collectives, sum_at_owner(): lax.all_to_all(parts, axis, split_axis=0, concat_axis=0, tiled=True)  34.8 us
    all_to_all x2, waiting for transfers between devices, exchange_both(): parts = lax.all_to_all(parts, axis, split_axis=0, concat_axis=0, tiled=True)  32.9 us
    all_to_all x1, other arithmetic, relocate(): lax.all_to_all(picked[0], ('gx', 'gy'), split_axis=0, concat_axis=1, tile...  26.3 us
    all_to_all x1, other arithmetic, relocate(): lax.all_to_all(picked[1], ('gx', 'gy'), split_axis=0, concat_axis=1, tile...  26.3 us
  transfers between devices with their start and end apart: 6, of which 3 were waited for; matrix products, arithmetic and copies ran while one was open for 34% of the time, Pallas kernels for 0%

commit v1 on v0

v1 whole, which is shorter than its diff:
```python
import jax
import jax.numpy as jnp
from jax import lax
from jax.experimental import pallas as pl
from jax.experimental.pallas import tpu as pltpu
from jax.sharding import PartitionSpec as P

MESH = pl.DeviceIdType.MESH
BF = jnp.bfloat16
F32 = jnp.float32

PLANE = ((1, 0), (0, 1), (3, 0), (0, 3), (1, 3), (3, 1), (2, 0), (0, 2), (1, 1), (3, 3), (2, 1), (2, 3), (1, 2), (3, 2), (2, 2))
LINE = ((0, 1), (1, 0), (3, 0), (1, 1), (3, 1), (2, 0), (2, 1))

ERFC_P = (2.326819970068386e-2, -1.387039388740657e-1, 3.687424674597105e-1, -5.824733027278666e-1, 6.210004621745983e-1,
          -4.944515323274145e-1, 3.404879937665872e-1, -2.741127028184656e-1, 5.638259427386472e-1)
ERFC_R = (-1.047766399936249e1, 1.297719955372516e1, -7.495518717768503e0, 2.921019019210786e0, -1.015265279202700e0,
          4.218463358204948e-1, -2.820767439740514e-1, 5.641895067754075e-1)
ERF_T = (7.853861353153693e-5, -8.010193625184903e-4, 5.188327685732524e-3, -2.685381193529856e-2, 1.128358514861418e-1,
         -3.761262582423300e-1, 1.128379165726710e0)


def poly(y, coefficients):
    total = jnp.full_like(y, coefficients[0])
    for c in coefficients[1:]:
        total = total * y + c
    return total


def erfc(v):
    size = jnp.maximum(jnp.abs(v), 0.5)
    q = 1.0 / size
    y = q * q
    tail = jnp.exp(-v * v) * q * jnp.where(size < 2.0, poly(y, ERFC_P), poly(y, ERFC_R))
    far = jnp.where(v < 0.0, 2.0 - tail, tail)
    near = 1.0 - v * poly(v * v, ERF_T)
    return jnp.where(jnp.abs(v) > 1.0, far, near)


def gelu(v):
    return 0.5 * v * erfc(v * -0.7071067811865476)


SEMS = ("s1u", "s1d", "s2u", "s2d", "s3u", "s3d", "s4u", "s4d", "agy", "agz", "agx", "agc", "agd", "rc", "ry", "rz", "rx", "wu", "wd", "tok")


def kernel(source, route, tokens, up, down, up2, down2, up_new, down_new, mixed, s1u, s1d, s3u, s3d,
           s2u, s2d, pu, pd, t, upv, downv, pre, hid, acc, sc, rc, ry, sz, rz, sx, rx, send, recv):
    gx, gy = lax.axis_index("gx"), lax.axis_index("gy")
    x, c = gx // 2, lax.rem(gx, 2)
    y, z = gy // 4, lax.rem(gy, 4)
    plane = [lax.rem(y + dy, 4) * 4 + lax.rem(z + dz, 4) for dy, dz in PLANE]
    line = [lax.rem(x + dx, 4) * 2 + lax.rem(c + dc, 2) for dx, dc in LINE]
    xs = [lax.rem(x + d, 4) for d in (1, 2, 3)]
    ys = [lax.rem(y + d, 4) for d in (1, 2, 3)]
    zs = [lax.rem(z + d, 4) for d in (1, 2, 3)]
    other = 1 - c
    at = {name: i for i, name in enumerate(SEMS)}

    def push(name, src, dst, where):
        pltpu.make_async_remote_copy(
            src_ref=src, dst_ref=dst, send_sem=send.at[at[name]], recv_sem=recv.at[at[name]], device_id=where, device_id_type=MESH
        ).start()

    def keep(name, src, dst):
        pltpu.make_async_copy(src, dst, recv.at[at[name]]).start()

    def got(name, ref):
        pltpu.make_async_copy(ref, ref, recv.at[at[name]]).wait()

    def sent(name, ref):
        pltpu.make_async_copy(ref, ref, send.at[at[name]]).wait()

    def cols(g):
        return pl.ds(pl.multiple_of(g * 1024, 1024), 1024)

    barrier = pltpu.get_barrier_semaphore()
    for p in plane:
        pl.semaphore_signal(barrier, inc=1, device_id={"gy": p}, device_id_type=MESH)
    for p in line:
        pl.semaphore_signal(barrier, inc=1, device_id={"gx": p}, device_id_type=MESH)
    pl.semaphore_wait(barrier, len(PLANE) + len(LINE))

    keep("tok", tokens, t.at[y, z, :, cols(gx)])
    for p in ys:
        push("agy", tokens, t.at[y, z, :, cols(gx)], {"gy": p * 4 + z})
    for p in line:
        push("s1d", down.at[:, :, :, cols(p)], s1d.at[gx], {"gx": p})
    keep("s1d", down.at[:, :, :, cols(gx)], s1d.at[gx])
    keep("wu", up2, upv)
    keep("wd", down2, downv)
    got("tok", tokens)
    got("agy", t.at[0, 0:3, :, pl.ds(0, 1024)])
    for p in zs:
        push("agz", t.at[:, z, :, cols(gx)], t.at[:, z, :, cols(gx)], {"gy": y * 4 + p})
    for p in plane:
        push("s1u", up.at[:, p], s1u.at[pl.ds(gy * 2, 2)], {"gy": p})
    keep("s1u", up.at[:, gy], s1u.at[pl.ds(gy * 2, 2)])
    got("agz", t.at[:, 0:3, :, pl.ds(0, 1024)])
    for p in xs:
        push("agx", t.at[:, :, :, cols(gx)], t.at[:, :, :, cols(gx)], {"gx": p * 2 + c})
    push("agc", t.at[:, :, :, cols(gx)], t.at[:, :, :, cols(gx)], {"gx": x * 2 + other})
    got("s1d", s1d)
    for p in plane:
        push("s2d", s1d.at[:, :, p], s2d.at[:, gy], {"gy": p})
    keep("s2d", s1d.at[:, :, gy], s2d.at[:, gy])
    got("s1u", s1u)
    for p in line:
        push("s2u", s1u.at[:, :, cols(p)], s2u.at[pl.ds(gx * 32, 32)], {"gx": p})
    keep("s2u", s1u.at[:, :, cols(gx)], s2u.at[pl.ds(gx * 32, 32)])
    got("agx", t.at[:, :, :, pl.ds(0, 3072)])
    for p in xs:
        push("agd", t.at[:, :, :, cols(p * 2 + c)], t.at[:, :, :, cols(p * 2 + c)], {"gx": x * 2 + other})
    got("agc", t.at[:, :, :, pl.ds(0, 1024)])
    got("agd", t.at[:, :, :, pl.ds(0, 3072)])

    got("wu", upv)
    pre[...] = jnp.zeros_like(pre)

    def first(k, carry):
        w = upv[:, pl.ds(pl.multiple_of(k * 1024, 1024), 1024)]

        def rows(m, inner):
            a = t[m, :, :, pl.ds(pl.multiple_of(k * 1024, 1024), 1024)].reshape(128, 1024)
            at_rows = pl.ds(pl.multiple_of(m * 128, 128), 128)
            pre[at_rows, :] += lax.dot_general(a, w, (((1,), (1,)), ((), ())), preferred_element_type=F32)
            return inner

        return lax.fori_loop(0, 4, rows, carry)

    lax.fori_loop(0, 8, first, 0)

    def act(m, carry):
        at_rows = pl.ds(pl.multiple_of(m * 64, 64), 64)
        hid[at_rows, :] = gelu(pre[at_rows, :]).astype(BF)
        return carry

    lax.fori_loop(0, 8, act, 0)

    def order(m, carry):
        at_rows = pl.ds(pl.multiple_of(m * 128, 128), 128)
        pick = jnp.where(route[at_rows, :] == lax.broadcasted_iota(jnp.int32, (128, 512), 1), 1.0, 0.0).astype(BF)
        pre[at_rows, :] = jnp.dot(pick, hid[...], preferred_element_type=F32)
        return carry

    lax.fori_loop(0, 4, order, 0)
    hid[...] = pre[...].astype(BF)
    got("wd", downv)

    for q in range(4):
        def theirs(m, carry):
            at_rows = pl.ds(pl.multiple_of(m * 128, 128), 128)
            sc[q, at_rows, :] = jnp.dot(hid[at_rows, :], downv[:, cols(q * 2 + other)], preferred_element_type=F32).astype(BF)
            return carry

        lax.fori_loop(0, 4, theirs, 0)
        push("rc", sc.at[q], rc.at[q], {"gx": x * 2 + other})

    def permute_down(n, carry):
        s = source[n]
        pd[n // 32, lax.rem(n // 2, 16), lax.rem(n, 2)] = s2d[s // 32, lax.rem(s // 2, 16), lax.rem(s, 2)]
        return carry

    got("s2d", s2d)
    lax.fori_loop(0, 256, permute_down, 0)
    for p in plane:
        push("s3d", pd.at[:, p], s3d.at[:, :, gy], {"gy": p})
    keep("s3d", pd.at[:, gy], s3d.at[:, :, gy])

    def mine(m, carry):
        at_rows = pl.ds(pl.multiple_of(lax.rem(m, 4) * 128, 128), 128)
        acc[m // 4, at_rows, :] = jnp.dot(hid[at_rows, :], downv[:, cols((m // 4) * 2 + c)], preferred_element_type=F32)
        return carry

    lax.fori_loop(0, 16, mine, 0)
    sent("rc", sc)
    got("rc", rc)

    def both(m, carry):
        q, at_rows = m // 8, pl.ds(pl.multiple_of(lax.rem(m, 8) * 64, 64), 64)
        total = acc[q, at_rows, :] + rc[q, at_rows, :].astype(F32)
        acc[q, at_rows, :] = total
        sc[q, at_rows, :] = total.astype(BF)
        return carry

    lax.fori_loop(0, 32, both, 0)
    for i, p in enumerate(ys):
        push("ry", sc.at[:, pl.ds(pl.multiple_of(p * 128, 128), 128), :], ry.at[i], {"gy": p * 4 + z})

    def permute_up(n, carry):
        pu[n] = s2u[source[n]]
        return carry

    got("s2u", s2u)
    lax.fori_loop(0, 256, permute_up, 0)
    for p in line:
        push("s3u", pu.at[pl.ds(p * 32, 32)], s3u.at[:, :, cols(gx)], {"gx": p})
    keep("s3u", pu.at[pl.ds(gx * 32, 32)], s3u.at[:, :, cols(gx)])

    got("s3d", s3d)
    for p in line:
        push("s4d", s3d.at[p], down_new.at[:, :, :, cols(gx)], {"gx": p})
    keep("s4d", s3d.at[gx], down_new.at[:, :, :, cols(gx)])

    got("ry", ry)

    def over_y(m, carry):
        q, r = m // 2, pl.multiple_of(lax.rem(m, 2) * 64, 64)
        at_rows = pl.ds(pl.multiple_of(y * 128 + r, 64), 64)
        total = acc[q, at_rows, :]
        for i in range(3):
            total = total + ry[i, q, pl.ds(r, 64), :].astype(F32)
        acc[q, at_rows, :] = total
        sz[q, pl.ds(r, 64), :] = total.astype(BF)
        return carry

    lax.fori_loop(0, 8, over_y, 0)
    for i, p in enumerate(zs):
        push("rz", sz.at[:, pl.ds(pl.multiple_of(p * 32, 32), 32), :], rz.at[i], {"gy": y * 4 + p})

    got("s3u", s3u)
    for p in plane:
        push("s4u", s3u.at[pl.ds(p * 2, 2)], up_new.at[:, gy], {"gy": p})
    keep("s4u", s3u.at[pl.ds(gy * 2, 2)], up_new.at[:, gy])

    got("rz", rz)
    here = pl.ds(pl.multiple_of(y * 128 + z * 32, 32), 32)

    def over_z(q, carry):
        total = acc[q, here, :]
        for i in range(3):
            total = total + rz[i, q].astype(F32)
        acc[q, here, :] = total
        sx[q] = total.astype(BF)
        return carry

    lax.fori_loop(0, 4, over_z, 0)
    for i, p in enumerate(xs):
        push("rx", sx.at[p], rx.at[i], {"gx": p * 2 + c})
    got("rx", rx)
    total = acc[x, here, :]
    for i in range(3):
        total = total + rx[i].astype(F32)
    mixed[...] = total.astype(BF)

    got("s4d", s1d)
    got("s4u", s1u)
    for name in ("s1u", "s2d", "s3d", "s4u"):
        sent(name, s1u.at[pl.ds(0, 30)])
    for name in ("s1d", "s2u", "s3u", "s4d"):
        sent(name, s1d.at[pl.ds(0, 7)])
    sent("agy", t.at[0, 0:3, :, pl.ds(0, 1024)])
    sent("agz", t.at[:, 0:3, :, pl.ds(0, 1024)])
    sent("agx", t.at[:, :, :, pl.ds(0, 3072)])
    sent("agc", t.at[:, :, :, pl.ds(0, 1024)])
    sent("agd", t.at[:, :, :, pl.ds(0, 3072)])
    sent("ry", ry)
    sent("rz", rz)
    sent("rx", rx)


def shards(tokens, up_old, down_old, old_slot, new_owner, hot_rank, route):
    new_slot = new_owner * 2 + hot_rank
    slots = lax.broadcasted_iota(jnp.int32, (256, 256), 0)
    source = jnp.sum(jnp.where(slots == new_slot[None, :], old_slot[None, :], 0), axis=1)
    up4, down4 = up_old.reshape(2, 16, 8, 8192), down_old.reshape(2, 16, 8, 8192)
    any_, vmem = pl.BlockSpec(memory_space=pl.ANY), pl.BlockSpec(memory_space=pltpu.VMEM)
    block = jax.ShapeDtypeStruct((2, 16, 8, 8192), BF)
    outs = pl.pallas_call(
        kernel,
        out_shape=(
            block, block, jax.ShapeDtypeStruct((32, 1024), BF),
            jax.ShapeDtypeStruct((32, 8, 8192), BF), jax.ShapeDtypeStruct((8, 2, 16, 8, 1024), BF),
            jax.ShapeDtypeStruct((32, 8, 8192), BF), jax.ShapeDtypeStruct((8, 2, 16, 8, 1024), BF),
        ),
        in_specs=[pl.BlockSpec(memory_space=pltpu.SMEM), vmem, any_, any_, any_, any_, any_],
        out_specs=(any_, any_, vmem, any_, any_, any_, any_),
        scratch_shapes=[
            pltpu.VMEM((256, 8, 1024), BF), pltpu.VMEM((8, 16, 2, 8, 1024), BF),
            pltpu.VMEM((256, 8, 1024), BF), pltpu.VMEM((8, 16, 2, 8, 1024), BF),
            pltpu.VMEM((4, 4, 32, 8192), BF), pltpu.VMEM((256, 8192), BF), pltpu.VMEM((256, 8192), BF),
            pltpu.VMEM((512, 256), F32), pltpu.VMEM((512, 256), BF),
            pltpu.VMEM((4, 512, 1024), F32), pltpu.VMEM((4, 512, 1024), BF), pltpu.VMEM((4, 512, 1024), BF),
            pltpu.VMEM((3, 4, 128, 1024), BF), pltpu.VMEM((4, 128, 1024), BF), pltpu.VMEM((3, 4, 32, 1024), BF),
            pltpu.VMEM((4, 32, 1024), BF), pltpu.VMEM((3, 32, 1024), BF),
            pltpu.SemaphoreType.DMA((len(SEMS),)), pltpu.SemaphoreType.DMA((len(SEMS),)),
        ],
        compiler_params=pltpu.CompilerParams(collective_id=0, has_side_effects=True, vmem_limit_bytes=67043328),
    )(source, route.reshape(512, 1), tokens, up4, down4, up_old, down_old)
    return outs[0].reshape(256, 8192), outs[1].reshape(256, 8192), outs[2]


def solution(mesh):
    in_specs = (P("gy", "gx"), P(("gx", "gy"), None), P(("gx", "gy"), None), P(), P(), P(), P())
    out_specs = (P(("gx", "gy"), None), P(("gx", "gy"), None), P("gy", "gx"))
    return jax.shard_map(shards, mesh=mesh, in_specs=in_specs, out_specs=out_specs, check_vma=False)
```

time: 572 us -> 304 us (0.53)
  the two profiles are of different devices: /device:TPU:0 before, /device:TPU:1 now
where the time goes in v1:
time: 304 us; the launch traced here: 299 us
  Pallas kernels  287 us (94%)
  local copies, waits for them, and re-layouts  8.97 us (3%)
    pallas_call x1, Pallas kernels, shards(): pl.pallas_call(kernel, out_shape=(block, block, jax.ShapeDtypeStruct((32,...  287 us
    unnamed x7, local copies, waits for them, and re-layouts  7.44 us

profile of v1, /device:TPU:1, one launch (start us, length us, event | category | flops | bytes accessed | tf_op | source)
XLA Modules:
  0.0 298.9 jit_solution(4470555406681734699)
XLA Ops:
  0.6 0.7 multiply_add_fusion
  1.3 1.4 select_reduce_fusion.source
  2.7 1.5 copy.11.route
  4.2 287.2 %shard_map.94 = (bf16[2,16,8,8192]{3,2,1,0:T(8,128)(2,1)}, bf16[2,16,8,8192]{3,2,1,0:T(8,128)(2,1)}, bf16[32,1024]{1,0:T(8,128)(2,1)}, bf16[32,8,8192]{2,1,0:T(8...) custom-call(s32[256]{0:T(256)} %select_reduce_fusion.source, ...), custom_call_target="tpu_custom_call" | custom-call | tf_op jit(solution)/shard_map/pallas_call | solution.py:269
  291.5 0.0 copy-start
  291.5 4.8 %copy.15 = bf16[256,8192]{1,0:T(8,128)(2,1)} copy(bf16[256,8192]{1,0:T(8,128)(2,1)} %bitcast.8) | data formatting | bytes 8388608
  296.3 0.0 copy-done
  296.3 0.0 copy-start.1
  296.3 2.0 copy.16
  298.3 0.0 copy-done.1
  298.3 0.6 copy.17
Async XLA Ops:
  291.5 4.8 %copy-start = (bf16[2,16,8,8192]{3,2,1,0:T(8,128)(2,1)S(1)}, bf16[2,16,8,8192]{3,2,1,0:T(8,128)(2,1)}, u32[]{:S(2)}) copy-start(bf16[2,16,8,8192]{3,2,1,0:T(8,128)(2,1)} %get-tuple-element.7) | copy-start | bytes 12582916
  296.3 2.0 copy-start.1

commit v2 on v0

v2 whole, which is shorter than its diff:
```python
import jax
import jax.numpy as jnp
from jax import lax
from jax.experimental import pallas as pl
from jax.experimental.pallas import tpu as pltpu
from jax.sharding import PartitionSpec as P

MESH = pl.DeviceIdType.MESH
BF = jnp.bfloat16
F32 = jnp.float32

PLANE = ((1, 0), (0, 1), (3, 0), (0, 3), (1, 3), (3, 1), (2, 0), (0, 2), (1, 1), (3, 3), (2, 1), (2, 3), (1, 2), (3, 2), (2, 2))
LINE = ((0, 1), (1, 0), (3, 0), (1, 1), (3, 1), (2, 0), (2, 1))

ERFC_P = (2.326819970068386e-2, -1.387039388740657e-1, 3.687424674597105e-1, -5.824733027278666e-1, 6.210004621745983e-1,
          -4.944515323274145e-1, 3.404879937665872e-1, -2.741127028184656e-1, 5.638259427386472e-1)
ERFC_R = (-1.047766399936249e1, 1.297719955372516e1, -7.495518717768503e0, 2.921019019210786e0, -1.015265279202700e0,
          4.218463358204948e-1, -2.820767439740514e-1, 5.641895067754075e-1)
ERF_T = (7.853861353153693e-5, -8.010193625184903e-4, 5.188327685732524e-3, -2.685381193529856e-2, 1.128358514861418e-1,
         -3.761262582423300e-1, 1.128379165726710e0)


def poly(y, coefficients):
    total = jnp.full_like(y, coefficients[0])
    for c in coefficients[1:]:
        total = total * y + c
    return total


def erfc(v):
    size = jnp.maximum(jnp.abs(v), 0.5)
    q = 1.0 / size
    y = q * q
    tail = jnp.exp(-v * v) * q * jnp.where(size < 2.0, poly(y, ERFC_P), poly(y, ERFC_R))
    far = jnp.where(v < 0.0, 2.0 - tail, tail)
    near = 1.0 - v * poly(v * v, ERF_T)
    return jnp.where(jnp.abs(v) > 1.0, far, near)


def gelu(v):
    return 0.5 * v * erfc(v * -0.7071067811865476)


NAMES = ("s1u", "s1d", "s2u", "s2d", "s3u", "s3d", "s4u", "s4d", "pc", "px")
SINGLE = ("tok", "agy", "agz", "hx", "hc", "hd", "ry", "rz")
AT = {(name, h): 2 * i + h for i, name in enumerate(NAMES) for h in (0, 1)}
AT.update({(name, 0): 2 * len(NAMES) + i for i, name in enumerate(SINGLE)})


def kernel(source, route, tokens, up, down, up_new, down_new, mixed, s1u, s1d, s3u, s3d,
           s2u, s2d, pu, pd, t, to, pr, pc, px, hid, hb, acc, sc, ry, sz, rz, send, recv):
    gx, gy = lax.axis_index("gx"), lax.axis_index("gy")
    x, c = gx // 2, lax.rem(gx, 2)
    y, z = gy // 4, lax.rem(gy, 4)
    plane = [lax.rem(y + dy, 4) * 4 + lax.rem(z + dz, 4) for dy, dz in PLANE]
    line = [lax.rem(x + dx, 4) * 2 + lax.rem(c + dc, 2) for dx, dc in LINE]
    xs = [lax.rem(x + d, 4) for d in (1, 3, 2)]
    ys = [lax.rem(y + d, 4) for d in (1, 3, 2)]
    zs = [lax.rem(z + d, 4) for d in (1, 3, 2)]
    other = 1 - c
    partner = {"gx": x * 2 + other}

    def push(name, h, src, dst, where):
        pltpu.make_async_remote_copy(
            src_ref=src, dst_ref=dst, send_sem=send.at[AT[name, h]], recv_sem=recv.at[AT[name, h]], device_id=where, device_id_type=MESH
        ).start()

    def keep(name, h, src, dst):
        pltpu.make_async_copy(src, dst, recv.at[AT[name, h]]).start()

    def got(name, h, ref):
        pltpu.make_async_copy(ref, ref, recv.at[AT[name, h]]).wait()

    def sent(name, h, ref):
        pltpu.make_async_copy(ref, ref, send.at[AT[name, h]]).wait()

    def cols(g):
        return pl.ds(pl.multiple_of(g * 1024, 1024), 1024)

    def lanes(g):
        return pl.ds(pl.multiple_of(g * 128, 128), 128)

    def rows(m, n):
        return pl.ds(pl.multiple_of(m * n, n), n)

    def s1u_(h):
        for p in plane:
            push("s1u", h, up.at[h, p], s1u.at[h, gy], {"gy": p})
        keep("s1u", h, up.at[h, gy], s1u.at[h, gy])

    def s1d_(h):
        for p in line:
            push("s1d", h, down.at[h, :, :, cols(p)], s1d.at[h, gx], {"gx": p})
        keep("s1d", h, down.at[h, :, :, cols(gx)], s1d.at[h, gx])

    def s2u_(h):
        got("s1u", h, s1u.at[h])
        for p in line:
            push("s2u", h, s1u.at[h, :, :, cols(p)], s2u.at[h, gx], {"gx": p})
        keep("s2u", h, s1u.at[h, :, :, cols(gx)], s2u.at[h, gx])

    def s2d_(h):
        got("s1d", h, s1d.at[h])
        for p in plane:
            push("s2d", h, s1d.at[h, :, p], s2d.at[h, :, gy], {"gy": p})
        keep("s2d", h, s1d.at[h, :, gy], s2d.at[h, :, gy])

    def permute(spread, picked, h):
        def one(m, carry):
            s = source[m * 2 + h]
            picked[h, m // 16, lax.rem(m, 16)] = spread[lax.rem(s, 2), s // 32, lax.rem(s // 2, 16)]
            return carry

        lax.fori_loop(0, 128, one, 0, unroll=4)

    def s3u_(h):
        for p in line:
            push("s3u", h, pu.at[h, p], s3u.at[h, :, :, cols(gx)], {"gx": p})
        keep("s3u", h, pu.at[h, gx], s3u.at[h, :, :, cols(gx)])

    def s3d_(h):
        for p in plane:
            push("s3d", h, pd.at[h, :, p], s3d.at[h, :, gy], {"gy": p})
        keep("s3d", h, pd.at[h, :, gy], s3d.at[h, :, gy])

    def s4u_(h):
        got("s3u", h, s3u.at[h])
        for p in plane:
            push("s4u", h, s3u.at[h, p], up_new.at[h, gy], {"gy": p})
        keep("s4u", h, s3u.at[h, gy], up_new.at[h, gy])

    def s4d_(h):
        got("s3d", h, s3d.at[h])
        for p in line:
            push("s4d", h, s3d.at[h, p], down_new.at[h, :, :, cols(gx)], {"gx": p})
        keep("s4d", h, s3d.at[h, gx], down_new.at[h, :, :, cols(gx)])

    def reorder_tokens():
        def some(m, carry):
            at_rows = rows(m, 128)
            pick = jnp.where(route[at_rows, :] == lax.broadcasted_iota(jnp.int32, (128, 512), 1), 1.0, 0.0).astype(BF)
            for n in range(2):
                part = t[:, :, :, pl.ds(n * 512, 512)].reshape(512, 512)
                to[at_rows, pl.ds(n * 512, 512)] = jnp.dot(pick, part, preferred_element_type=F32).astype(BF)
            return carry

        lax.fori_loop(0, 4, some, 0)

    def first_product(h):
        def some(q, carry):
            w = s2u[h, pl.ds(q * 2, 2)].astype(F32).reshape(256, 1024).astype(BF)
            for m in range(2):
                a = to[pl.ds(m * 256, 256), :]
                pr[h, q, pl.ds(m * 256, 256), :] = lax.dot_general(a, w, (((1,), (1,)), ((), ())), preferred_element_type=F32)
            return carry

        lax.fori_loop(0, 4, some, 0)
        push("pc", h, pr.at[h, :, :, lanes(other)], pc.at[h], partner)

    def over_cores(h):
        got("pc", h, pc.at[h])

        def some(m, carry):
            q, at_rows = m // 4, rows(lax.rem(m, 4), 128)
            pc[h, q, at_rows, :] = pc[h, q, at_rows, :] + pr[h, q, at_rows, lanes(c)]
            return carry

        lax.fori_loop(0, 16, some, 0)
        for i, p in enumerate(xs):
            push("px", h, pc.at[h, p], px.at[h, i], {"gx": p * 2 + c})

    def activate():
        for h in (0, 1):
            got("px", h, px.at[h])

            def some(m, carry):
                at_rows = rows(m, 128)
                total = pc[h, x, at_rows, :] + px[h, 0, at_rows, :] + px[h, 1, at_rows, :] + px[h, 2, at_rows, :]
                hb[gx, at_rows, pl.ds(h * 128, 128)] = gelu(total).astype(BF)
                return carry

            lax.fori_loop(0, 4, some, 0)
        for p in xs:
            push("hx", 0, hb.at[gx], hb.at[gx], {"gx": p * 2 + c})
        push("hc", 0, hb.at[gx], hb.at[gx], partner)

    def share_hidden():
        got("hx", 0, hb.at[pl.ds(0, 3)])
        for p in xs:
            push("hd", 0, hb.at[p * 2 + c], hb.at[p * 2 + c], partner)

    def second_product():
        got("hc", 0, hb.at[0])
        got("hd", 0, hb.at[pl.ds(0, 3)])
        acc[...] = jnp.zeros_like(acc)

        def some(q, carry):
            w = s2d[:, q].astype(F32).reshape(256, 1024).astype(BF)
            for m in range(2):
                for n in range(2):
                    at_rows, at_cols = pl.ds(m * 256, 256), pl.ds(n * 512, 512)
                    part = jnp.dot(hb[q, at_rows, :], w[:, n * 512 : n * 512 + 512], preferred_element_type=F32)
                    acc[at_rows, at_cols] += part
            return carry

        lax.fori_loop(0, 8, some, 0)

        def rounded(m, carry):
            at_rows = rows(m, 32)
            sc[at_rows, :] = acc[at_rows, :].astype(BF)
            return carry

        lax.fori_loop(0, 16, rounded, 0)
        for i, p in enumerate(ys):
            push("ry", 0, sc.at[rows(p, 128), :], ry.at[i], {"gy": p * 4 + z})

    def over_y():
        got("ry", 0, ry)

        def some(m, carry):
            at_rows = pl.ds(pl.multiple_of(y * 128 + m * 32, 32), 32)
            total = acc[at_rows, :]
            for i in range(3):
                total = total + ry[i, rows(m, 32), :].astype(F32)
            acc[at_rows, :] = total
            sz[rows(m, 32), :] = total.astype(BF)
            return carry

        lax.fori_loop(0, 4, some, 0)
        for i, p in enumerate(zs):
            push("rz", 0, sz.at[rows(p, 32), :], rz.at[i], {"gy": y * 4 + p})

    def over_z():
        got("rz", 0, rz)
        total = acc[pl.ds(pl.multiple_of(y * 128 + z * 32, 32), 32), :]
        for i in range(3):
            total = total + rz[i].astype(F32)
        mixed[...] = total.astype(BF)

    barrier = pltpu.get_barrier_semaphore()
    for p in plane:
        pl.semaphore_signal(barrier, inc=1, device_id={"gy": p}, device_id_type=MESH)
    for p in line:
        pl.semaphore_signal(barrier, inc=1, device_id={"gx": p}, device_id_type=MESH)
    pl.semaphore_wait(barrier, len(PLANE) + len(LINE))

    keep("tok", 0, tokens, t.at[y, z])
    for p in ys:
        push("agy", 0, tokens, t.at[y, z], {"gy": p * 4 + z})
    s1u_(0)
    s1d_(0)
    s1d_(1)
    got("tok", 0, tokens)
    got("agy", 0, t.at[0, pl.ds(0, 3)])
    for p in zs:
        push("agz", 0, t.at[:, z], t.at[:, z], {"gy": y * 4 + p})
    s1u_(1)
    s2u_(0)
    s2d_(0)
    got("agz", 0, t.at[:, pl.ds(0, 3)])
    reorder_tokens()
    s2d_(1)
    s2u_(1)
    got("s2u", 0, s2u.at[0])
    first_product(0)
    over_cores(0)
    got("s2u", 1, s2u.at[1])
    first_product(1)
    permute(s2u, pu, 0)
    over_cores(1)
    s3u_(0)
    got("s2d", 0, s2d.at[0])
    got("s2d", 1, s2d.at[1])
    permute(s2d, pd, 0)
    s3d_(0)
    permute(s2d, pd, 1)
    s3d_(1)
    activate()
    permute(s2u, pu, 1)
    s3u_(1)
    s4u_(0)
    share_hidden()
    second_product()
    s4d_(0)
    over_y()
    s4u_(1)
    s4d_(1)
    over_z()

    for h in (0, 1):
        got("s4u", h, s1u.at[h])
        got("s4d", h, s1d.at[h])
    for h in (0, 1):
        for name in ("s1u", "s2d", "s3d", "s4u"):
            sent(name, h, s1u.at[h, pl.ds(0, 15)])
        for name in ("s1d", "s2u", "s3u", "s4d"):
            sent(name, h, s1d.at[h, pl.ds(0, 7)])
        sent("pc", h, pc.at[h])
        sent("px", h, px.at[h])
    sent("agy", 0, t.at[0, pl.ds(0, 3)])
    sent("agz", 0, t.at[:, pl.ds(0, 3)])
    sent("hx", 0, hb.at[pl.ds(0, 3)])
    sent("hc", 0, hb.at[0])
    sent("hd", 0, hb.at[pl.ds(0, 3)])
    sent("ry", 0, ry)
    sent("rz", 0, rz)


def shards(tokens, up_old, down_old, old_slot, new_owner, hot_rank, route):
    new_slot = new_owner * 2 + hot_rank
    slots = lax.broadcasted_iota(jnp.int32, (256, 256), 0)
    source = jnp.sum(jnp.where(slots == new_slot[None, :], old_slot[None, :], 0), axis=1)
    up4, down4 = up_old.reshape(2, 16, 8, 8192), down_old.reshape(2, 16, 8, 8192)
    any_, vmem = pl.BlockSpec(memory_space=pl.ANY), pl.BlockSpec(memory_space=pltpu.VMEM)
    block = jax.ShapeDtypeStruct((2, 16, 8, 8192), BF)
    tiles = jax.ShapeDtypeStruct((2, 8, 16, 8, 1024), BF)
    outs = pl.pallas_call(
        kernel,
        out_shape=(block, block, jax.ShapeDtypeStruct((32, 1024), BF), block, tiles, block, tiles),
        in_specs=[pl.BlockSpec(memory_space=pltpu.SMEM), vmem, any_, any_, any_],
        out_specs=(any_, any_, vmem, any_, any_, any_, any_),
        scratch_shapes=[
            pltpu.VMEM((2, 8, 16, 8, 1024), BF), pltpu.VMEM((2, 8, 16, 8, 1024), BF),
            pltpu.VMEM((2, 8, 16, 8, 1024), BF), pltpu.VMEM((2, 8, 16, 8, 1024), BF),
            pltpu.VMEM((4, 4, 32, 1024), BF), pltpu.VMEM((512, 1024), BF),
            pltpu.VMEM((2, 4, 512, 256), F32), pltpu.VMEM((2, 4, 512, 128), F32), pltpu.VMEM((2, 3, 512, 128), F32),
            pltpu.VMEM((512, 256), BF), pltpu.VMEM((8, 512, 256), BF),
            pltpu.VMEM((512, 1024), F32), pltpu.VMEM((512, 1024), BF),
            pltpu.VMEM((3, 128, 1024), BF), pltpu.VMEM((128, 1024), BF), pltpu.VMEM((3, 32, 1024), BF),
            pltpu.SemaphoreType.DMA((len(AT),)), pltpu.SemaphoreType.DMA((len(AT),)),
        ],
        compiler_params=pltpu.CompilerParams(collective_id=0, has_side_effects=True, vmem_limit_bytes=67043328),
    )(source, route.reshape(512, 1), tokens, up4, down4)
    return outs[0].reshape(256, 8192), outs[1].reshape(256, 8192), outs[2]


def solution(mesh):
    in_specs = (P("gy", "gx"), P(("gx", "gy"), None), P(("gx", "gy"), None), P(), P(), P(), P())
    out_specs = (P(("gx", "gy"), None), P(("gx", "gy"), None), P("gy", "gx"))
    return jax.shard_map(shards, mesh=mesh, in_specs=in_specs, out_specs=out_specs, check_vma=False)
```

time: 572 us -> 259 us (0.45)
  the two profiles are of different devices: /device:TPU:0 before, /device:TPU:1 now
where the time goes in v2:
time: 259 us; the launch traced here: 258 us
  Pallas kernels  247 us (95%)
  local copies, waits for them, and re-layouts  8.97 us (3%)
    pallas_call x1, Pallas kernels, shards(): pl.pallas_call(kernel, out_shape=(block, block, jax.ShapeDtypeStruct((32,...  247 us
    unnamed x7, local copies, waits for them, and re-layouts  7.44 us

profile of v2, /device:TPU:1, one launch (start us, length us, event | category | flops | bytes accessed | tf_op | source)
XLA Modules:
  0.0 258.5 jit_solution(3241090138297300916)
XLA Ops:
  0.6 0.7 multiply_add_fusion
  1.3 1.4 select_reduce_fusion.source
  2.7 1.5 copy.11.route
  4.2 246.8 %shard_map.94 = (bf16[2,16,8,8192]{3,2,1,0:T(8,128)(2,1)}, bf16[2,16,8,8192]{3,2,1,0:T(8,128)(2,1)}, bf16[32,1024]{1,0:T(8,128)(2,1)}, bf16[2,16,8,8192]{3,2,1,0...) custom-call(s32[256]{0:T(256)} %select_reduce_fusion.source, ...), custom_call_target="tpu_custom_call" | custom-call | tf_op jit(solution)/shard_map/pallas_call | solution.py:317
  251.0 0.0 copy-start
  251.0 4.8 %copy.15 = bf16[256,8192]{1,0:T(8,128)(2,1)} copy(bf16[256,8192]{1,0:T(8,128)(2,1)} %bitcast.8) | data formatting | bytes 8388608
  255.8 0.0 copy-done
  255.8 0.0 copy-start.1
  255.8 2.0 copy.16
  257.8 0.0 copy-done.1
  257.8 0.6 copy.17
Async XLA Ops:
  251.0 4.8 %copy-start = (bf16[2,16,8,8192]{3,2,1,0:T(8,128)(2,1)S(1)}, bf16[2,16,8,8192]{3,2,1,0:T(8,128)(2,1)}, u32[]{:S(2)}) copy-start(bf16[2,16,8,8192]{3,2,1,0:T(8,128)(2,1)} %get-tuple-element.7) | copy-start | bytes 12582916
  255.8 2.0 copy-start.1

commit v3 on v2

--- a/solution.py
+++ b/solution.py
@@ -41,6 +41,7 @@
     return 0.5 * v * erfc(v * -0.7071067811865476)
 
 
+HALF = (0, 1)
 NAMES = ("s1u", "s1d", "s2u", "s2d", "s3u", "s3d", "s4u", "s4d", "pc", "px")
 SINGLE = ("tok", "agy", "agz", "hx", "hc", "hd", "ry", "rz")
 AT = {(name, h): 2 * i + h for i, name in enumerate(NAMES) for h in (0, 1)}
@@ -48,7 +49,7 @@
 
 
 def kernel(source, route, tokens, up, down, up_new, down_new, mixed, s1u, s1d, s3u, s3d,
-           s2u, s2d, pu, pd, t, to, pr, pc, px, hid, hb, acc, sc, ry, sz, rz, send, recv):
+           s2u, s2d, pu, pd, t, to, pr, pc, pb, px, hb, acc, sc, ry, sz, rz, send, recv):
     gx, gy = lax.axis_index("gx"), lax.axis_index("gy")
     x, c = gx // 2, lax.rem(gx, 2)
     y, z = gy // 4, lax.rem(gy, 4)
@@ -77,6 +78,12 @@
     def cols(g):
         return pl.ds(pl.multiple_of(g * 1024, 1024), 1024)
 
+    def wide(k):
+        return pl.ds(k * 4096, 4096)
+
+    def four(k):
+        return pl.ds(k * 4, 4)
+
     def lanes(g):
         return pl.ds(pl.multiple_of(g * 128, 128), 128)
 
@@ -84,8 +91,9 @@
         return pl.ds(pl.multiple_of(m * n, n), n)
 
     def s1u_(h):
-        for p in plane:
-            push("s1u", h, up.at[h, p], s1u.at[h, gy], {"gy": p})
+        for k in HALF:
+            for p in plane:
+                push("s1u", h, up.at[h, p, :, wide(k)], s1u.at[h, gy, :, wide(k)], {"gy": p})
         keep("s1u", h, up.at[h, gy], s1u.at[h, gy])
 
     def s1d_(h):
@@ -101,32 +109,45 @@
 
     def s2d_(h):
         got("s1d", h, s1d.at[h])
-        for p in plane:
-            push("s2d", h, s1d.at[h, :, p], s2d.at[h, :, gy], {"gy": p})
+        for k in HALF:
+            for p in plane:
+                push("s2d", h, s1d.at[h, four(k), p], s2d.at[h, four(k), gy], {"gy": p})
         keep("s2d", h, s1d.at[h, :, gy], s2d.at[h, :, gy])
 
-    def permute(spread, picked, h):
-        def one(m, carry):
-            s = source[m * 2 + h]
-            picked[h, m // 16, lax.rem(m, 16)] = spread[lax.rem(s, 2), s // 32, lax.rem(s // 2, 16)]
-            return carry
-
-        lax.fori_loop(0, 128, one, 0, unroll=4)
+    def pick(spread, picked, h, g, r):
+        s = source[(g * 16 + r) * 2 + h]
+        picked[h, g, r] = spread[lax.rem(s, 2), s // 32, lax.rem(s // 2, 16)]
 
     def s3u_(h):
-        for p in line:
-            push("s3u", h, pu.at[h, p], s3u.at[h, :, :, cols(gx)], {"gx": p})
-        keep("s3u", h, pu.at[h, gx], s3u.at[h, :, :, cols(gx)])
+        for p in [*line, gx]:
+            def one(r, carry):
+                pick(s2u, pu, h, p, r)
+                return carry
+
+            lax.fori_loop(0, 16, one, 0, unroll=4)
+            if p is gx:
+                keep("s3u", h, pu.at[h, p], s3u.at[h, :, :, cols(gx)])
+            else:
+                push("s3u", h, pu.at[h, p], s3u.at[h, :, :, cols(gx)], {"gx": p})
 
     def s3d_(h):
-        for p in plane:
-            push("s3d", h, pd.at[h, :, p], s3d.at[h, :, gy], {"gy": p})
-        keep("s3d", h, pd.at[h, :, gy], s3d.at[h, :, gy])
+        for k in HALF:
+            for p in [*plane, gy]:
+                def one(g, carry):
+                    pick(s2d, pd, h, k * 4 + g, p)
+                    return carry
+
+                lax.fori_loop(0, 4, one, 0, unroll=4)
+                if p is gy:
+                    keep("s3d", h, pd.at[h, four(k), p], s3d.at[h, four(k), gy])
+                else:
+                    push("s3d", h, pd.at[h, four(k), p], s3d.at[h, four(k), gy], {"gy": p})
 
     def s4u_(h):
         got("s3u", h, s3u.at[h])
-        for p in plane:
-            push("s4u", h, s3u.at[h, p], up_new.at[h, gy], {"gy": p})
+        for k in HALF:
+            for p in plane:
+                push("s4u", h, s3u.at[h, p, :, wide(k)], up_new.at[h, gy, :, wide(k)], {"gy": p})
         keep("s4u", h, s3u.at[h, gy], up_new.at[h, gy])
 
     def s4d_(h):
@@ -162,12 +183,14 @@
 
         def some(m, carry):
             q, at_rows = m // 4, rows(lax.rem(m, 4), 128)
-            pc[h, q, at_rows, :] = pc[h, q, at_rows, :] + pr[h, q, at_rows, lanes(c)]
+            total = pc[h, q, at_rows, :] + pr[h, q, at_rows, lanes(c)]
+            pc[h, q, at_rows, :] = total
+            pb[h, q, at_rows, :] = total.astype(BF)
             return carry
 
         lax.fori_loop(0, 16, some, 0)
         for i, p in enumerate(xs):
-            push("px", h, pc.at[h, p], px.at[h, i], {"gx": p * 2 + c})
+            push("px", h, pb.at[h, p], px.at[h, i], {"gx": p * 2 + c})
 
     def activate():
         for h in (0, 1):
@@ -175,7 +198,9 @@
 
             def some(m, carry):
                 at_rows = rows(m, 128)
-                total = pc[h, x, at_rows, :] + px[h, 0, at_rows, :] + px[h, 1, at_rows, :] + px[h, 2, at_rows, :]
+                total = pc[h, x, at_rows, :]
+                for i in range(3):
+                    total = total + px[h, i, at_rows, :].astype(F32)
                 hb[gx, at_rows, pl.ds(h * 128, 128)] = gelu(total).astype(BF)
                 return carry
 
@@ -266,17 +291,13 @@
     over_cores(0)
     got("s2u", 1, s2u.at[1])
     first_product(1)
-    permute(s2u, pu, 0)
     over_cores(1)
     s3u_(0)
     got("s2d", 0, s2d.at[0])
     got("s2d", 1, s2d.at[1])
-    permute(s2d, pd, 0)
     s3d_(0)
-    permute(s2d, pd, 1)
     s3d_(1)
     activate()
-    permute(s2u, pu, 1)
     s3u_(1)
     s4u_(0)
     share_hidden()
@@ -323,8 +344,8 @@
             pltpu.VMEM((2, 8, 16, 8, 1024), BF), pltpu.VMEM((2, 8, 16, 8, 1024), BF),
             pltpu.VMEM((2, 8, 16, 8, 1024), BF), pltpu.VMEM((2, 8, 16, 8, 1024), BF),
             pltpu.VMEM((4, 4, 32, 1024), BF), pltpu.VMEM((512, 1024), BF),
-            pltpu.VMEM((2, 4, 512, 256), F32), pltpu.VMEM((2, 4, 512, 128), F32), pltpu.VMEM((2, 3, 512, 128), F32),
-            pltpu.VMEM((512, 256), BF), pltpu.VMEM((8, 512, 256), BF),
+            pltpu.VMEM((2, 4, 512, 256), F32), pltpu.VMEM((2, 4, 512, 128), F32), pltpu.VMEM((2, 4, 512, 128), BF), pltpu.VMEM((2, 3, 512, 128), BF),
+            pltpu.VMEM((8, 512, 256), BF),
             pltpu.VMEM((512, 1024), F32), pltpu.VMEM((512, 1024), BF),
             pltpu.VMEM((3, 128, 1024), BF), pltpu.VMEM((128, 1024), BF), pltpu.VMEM((3, 32, 1024), BF),
             pltpu.SemaphoreType.DMA((len(AT),)), pltpu.SemaphoreType.DMA((len(AT),)),

time: 259 us -> 242 us (0.934); the launches traced: 258 us -> 239 us
  Pallas kernels: 247 us -> 227 us
    pallas_call x1, Pallas kernels: 247 us -> 227 us  [shards(): pl.pallas_call(kernel, out_shape=(block, block, jax.ShapeDtypeStruct((32,...]
where the time goes in v3:
time: 242 us; the launch traced here: 239 us
  Pallas kernels  227 us (94%)
  local copies, waits for them, and re-layouts  8.97 us (4%)
    pallas_call x1, Pallas kernels, shards(): pl.pallas_call(kernel, out_shape=(block, block, jax.ShapeDtypeStruct((32,...  227 us
    unnamed x7, local copies, waits for them, and re-layouts  7.44 us

profile of v3, /device:TPU:1, one launch (start us, length us, event | category | flops | bytes accessed | tf_op | source)
XLA Modules:
  0.0 238.7 jit_solution(4418454479472273132)
XLA Ops:
  0.6 0.7 multiply_add_fusion
  1.3 1.4 select_reduce_fusion.source
  2.7 1.5 copy.11.route
  4.2 227.0 %shard_map.94 = (bf16[2,16,8,8192]{3,2,1,0:T(8,128)(2,1)}, bf16[2,16,8,8192]{3,2,1,0:T(8,128)(2,1)}, bf16[32,1024]{1,0:T(8,128)(2,1)}, bf16[2,16,8,8192]{3,2,1,0...) custom-call(s32[256]{0:T(256)} %select_reduce_fusion.source, ...), custom_call_target="tpu_custom_call" | custom-call | tf_op jit(solution)/shard_map/pallas_call | solution.py:338
  231.2 0.0 copy-start
  231.2 4.8 %copy.15 = bf16[256,8192]{1,0:T(8,128)(2,1)} copy(bf16[256,8192]{1,0:T(8,128)(2,1)} %bitcast.8) | data formatting | bytes 8388608
  236.0 0.0 copy-done
  236.0 0.0 copy-start.1
  236.0 2.0 copy.16
  238.0 0.0 copy-done.1
  238.0 0.6 copy.17
Async XLA Ops:
  231.2 4.8 %copy-start = (bf16[2,16,8,8192]{3,2,1,0:T(8,128)(2,1)S(1)}, bf16[2,16,8,8192]{3,2,1,0:T(8,128)(2,1)}, u32[]{:S(2)}) copy-start(bf16[2,16,8,8192]{3,2,1,0:T(8,128)(2,1)} %get-tuple-element.7) | copy-start | bytes 12582916
  236.0 2.0 copy-start.1

commit v4 on v3

--- a/solution.py
+++ b/solution.py
@@ -81,6 +81,9 @@
     def wide(k):
         return pl.ds(k * 4096, 4096)
 
+    def eight(k):
+        return pl.ds(k * 8, 8)
+
     def four(k):
         return pl.ds(k * 4, 4)
 
@@ -97,14 +100,16 @@
         keep("s1u", h, up.at[h, gy], s1u.at[h, gy])
 
     def s1d_(h):
-        for p in line:
-            push("s1d", h, down.at[h, :, :, cols(p)], s1d.at[h, gx], {"gx": p})
+        for k in HALF:
+            for p in line:
+                push("s1d", h, down.at[h, eight(k), :, cols(p)], s1d.at[h, gx, eight(k)], {"gx": p})
         keep("s1d", h, down.at[h, :, :, cols(gx)], s1d.at[h, gx])
 
     def s2u_(h):
         got("s1u", h, s1u.at[h])
-        for p in line:
-            push("s2u", h, s1u.at[h, :, :, cols(p)], s2u.at[h, gx], {"gx": p})
+        for k in HALF:
+            for p in line:
+                push("s2u", h, s1u.at[h, eight(k), :, cols(p)], s2u.at[h, gx, eight(k)], {"gx": p})
         keep("s2u", h, s1u.at[h, :, :, cols(gx)], s2u.at[h, gx])
 
     def s2d_(h):
@@ -152,17 +157,18 @@
 
     def s4d_(h):
         got("s3d", h, s3d.at[h])
-        for p in line:
-            push("s4d", h, s3d.at[h, p], down_new.at[h, :, :, cols(gx)], {"gx": p})
+        for k in HALF:
+            for p in line:
+                push("s4d", h, s3d.at[h, p, eight(k)], down_new.at[h, eight(k), :, cols(gx)], {"gx": p})
         keep("s4d", h, s3d.at[h, gx], down_new.at[h, :, :, cols(gx)])
 
     def reorder_tokens():
         def some(m, carry):
             at_rows = rows(m, 128)
-            pick = jnp.where(route[at_rows, :] == lax.broadcasted_iota(jnp.int32, (128, 512), 1), 1.0, 0.0).astype(BF)
+            pick = jnp.where(route[:, at_rows] == lax.broadcasted_iota(jnp.int32, (512, 128), 0), 1.0, 0.0).astype(BF)
             for n in range(2):
                 part = t[:, :, :, pl.ds(n * 512, 512)].reshape(512, 512)
-                to[at_rows, pl.ds(n * 512, 512)] = jnp.dot(pick, part, preferred_element_type=F32).astype(BF)
+                to[at_rows, pl.ds(n * 512, 512)] = lax.dot_general(pick, part, (((0,), (0,)), ((), ())), preferred_element_type=F32).astype(BF)
             return carry
 
         lax.fori_loop(0, 4, some, 0)
@@ -248,7 +254,7 @@
             for i in range(3):
                 total = total + ry[i, rows(m, 32), :].astype(F32)
             acc[at_rows, :] = total
-            sz[rows(m, 32), :] = total.astype(BF)
+            sz[rows(m, 32), :] = total
             return carry
 
         lax.fori_loop(0, 4, some, 0)
@@ -259,7 +265,7 @@
         got("rz", 0, rz)
         total = acc[pl.ds(pl.multiple_of(y * 128 + z * 32, 32), 32), :]
         for i in range(3):
-            total = total + rz[i].astype(F32)
+            total = total + rz[i]
         mixed[...] = total.astype(BF)
 
     barrier = pltpu.get_barrier_semaphore()
@@ -303,9 +309,9 @@
     share_hidden()
     second_product()
     s4d_(0)
-    over_y()
     s4u_(1)
     s4d_(1)
+    over_y()
     over_z()
 
     for h in (0, 1):
@@ -328,9 +334,9 @@
 
 
 def shards(tokens, up_old, down_old, old_slot, new_owner, hot_rank, route):
-    new_slot = new_owner * 2 + hot_rank
     slots = lax.broadcasted_iota(jnp.int32, (256, 256), 0)
-    source = jnp.sum(jnp.where(slots == new_slot[None, :], old_slot[None, :], 0), axis=1)
+    here = (slots // 2 == new_owner[None, :]) & (slots % 2 == hot_rank[None, :])
+    source = jnp.sum(jnp.where(here, old_slot[None, :], 0), axis=1)
     up4, down4 = up_old.reshape(2, 16, 8, 8192), down_old.reshape(2, 16, 8, 8192)
     any_, vmem = pl.BlockSpec(memory_space=pl.ANY), pl.BlockSpec(memory_space=pltpu.VMEM)
     block = jax.ShapeDtypeStruct((2, 16, 8, 8192), BF)
@@ -347,11 +353,11 @@
             pltpu.VMEM((2, 4, 512, 256), F32), pltpu.VMEM((2, 4, 512, 128), F32), pltpu.VMEM((2, 4, 512, 128), BF), pltpu.VMEM((2, 3, 512, 128), BF),
             pltpu.VMEM((8, 512, 256), BF),
             pltpu.VMEM((512, 1024), F32), pltpu.VMEM((512, 1024), BF),
-            pltpu.VMEM((3, 128, 1024), BF), pltpu.VMEM((128, 1024), BF), pltpu.VMEM((3, 32, 1024), BF),
+            pltpu.VMEM((3, 128, 1024), BF), pltpu.VMEM((128, 1024), F32), pltpu.VMEM((3, 32, 1024), F32),
             pltpu.SemaphoreType.DMA((len(AT),)), pltpu.SemaphoreType.DMA((len(AT),)),
         ],
         compiler_params=pltpu.CompilerParams(collective_id=0, has_side_effects=True, vmem_limit_bytes=67043328),
-    )(source, route.reshape(512, 1), tokens, up4, down4)
+    )(source, route.reshape(1, 512), tokens, up4, down4)
     return outs[0].reshape(256, 8192), outs[1].reshape(256, 8192), outs[2]
 
 

time: 242 us -> 238 us (0.983)
  no operation moved by 1% of the time
where the time goes in v4:
time: 238 us; the launch traced here: 236 us
  Pallas kernels  226 us (95%)
  local copies, waits for them, and re-layouts  7.44 us (3%)
    pallas_call x1, Pallas kernels, shards(): pl.pallas_call(kernel, out_shape=(block, block, jax.ShapeDtypeStruct((32,...  226 us
    unnamed x7, local copies, waits for them, and re-layouts  7.44 us

profile of v4, /device:TPU:1, one launch (start us, length us, event | category | flops | bytes accessed | tf_op | source)
XLA Modules:
  0.0 236.1 jit_solution(486284897594808368)
XLA Ops:
  0.7 1.6 select_reduce_fusion.source
  2.3 226.3 %shard_map.94 = (bf16[2,16,8,8192]{3,2,1,0:T(8,128)(2,1)}, bf16[2,16,8,8192]{3,2,1,0:T(8,128)(2,1)}, bf16[32,1024]{1,0:T(8,128)(2,1)}, bf16[2,16,8,8192]{3,2,1,0...) custom-call(s32[256]{0:T(256)} %select_reduce_fusion.source, ...), custom_call_target="tpu_custom_call" | custom-call | tf_op jit(solution)/shard_map/pallas_call | solution.py:344
  228.6 0.0 copy-start
  228.6 4.8 %copy.13 = bf16[256,8192]{1,0:T(8,128)(2,1)} copy(bf16[256,8192]{1,0:T(8,128)(2,1)} %bitcast.8) | data formatting | bytes 8388608
  233.4 0.0 copy-done
  233.4 0.0 copy-start.1
  233.4 2.0 copy.14
  235.4 0.0 copy-done.1
  235.4 0.6 copy.15
  (3 shorter events, 0.0 us)
Async XLA Ops:
  228.6 4.8 %copy-start = (bf16[2,16,8,8192]{3,2,1,0:T(8,128)(2,1)S(1)}, bf16[2,16,8,8192]{3,2,1,0:T(8,128)(2,1)}, u32[]{:S(2)}) copy-start(bf16[2,16,8,8192]{3,2,1,0:T(8,128)(2,1)} %get-tuple-element.7) | copy-start | bytes 12582916
  233.4 2.0 copy-start.1

commit v5 on v4

--- a/solution.py
+++ b/solution.py
@@ -124,16 +124,17 @@
         picked[h, g, r] = spread[lax.rem(s, 2), s // 32, lax.rem(s // 2, 16)]
 
     def s3u_(h):
-        for p in [*line, gx]:
-            def one(r, carry):
-                pick(s2u, pu, h, p, r)
-                return carry
-
-            lax.fori_loop(0, 16, one, 0, unroll=4)
-            if p is gx:
-                keep("s3u", h, pu.at[h, p], s3u.at[h, :, :, cols(gx)])
-            else:
-                push("s3u", h, pu.at[h, p], s3u.at[h, :, :, cols(gx)], {"gx": p})
+        for k in HALF:
+            for p in [*line, gx]:
+                def one(r, carry):
+                    pick(s2u, pu, h, p, k * 8 + r)
+                    return carry
+
+                lax.fori_loop(0, 8, one, 0, unroll=4)
+                if p is gx:
+                    keep("s3u", h, pu.at[h, p, eight(k)], s3u.at[h, eight(k), :, cols(gx)])
+                else:
+                    push("s3u", h, pu.at[h, p, eight(k)], s3u.at[h, eight(k), :, cols(gx)], {"gx": p})
 
     def s3d_(h):
         for k in HALF:

time: 238 us -> 238 us (level)
  no operation moved by 1% of the time
where the time goes in v5:
time: 238 us; the launch traced here: 236 us
  Pallas kernels  226 us (95%)
  local copies, waits for them, and re-layouts  7.44 us (3%)
    pallas_call x1, Pallas kernels, shards(): pl.pallas_call(kernel, out_shape=(block, block, jax.ShapeDtypeStruct((32,...  226 us
    unnamed x7, local copies, waits for them, and re-layouts  7.44 us

profile of v5, /device:TPU:1, one launch (start us, length us, event | category | flops | bytes accessed | tf_op | source)
XLA Modules:
  0.0 236.1 jit_solution(9518791939847432476)
XLA Ops:
  0.7 1.6 select_reduce_fusion.source
  2.3 226.3 %shard_map.94 = (bf16[2,16,8,8192]{3,2,1,0:T(8,128)(2,1)}, bf16[2,16,8,8192]{3,2,1,0:T(8,128)(2,1)}, bf16[32,1024]{1,0:T(8,128)(2,1)}, bf16[2,16,8,8192]{3,2,1,0...) custom-call(s32[256]{0:T(256)} %select_reduce_fusion.source, ...), custom_call_target="tpu_custom_call" | custom-call | tf_op jit(solution)/shard_map/pallas_call | solution.py:345
  228.6 0.0 copy-start
  228.6 4.8 %copy.13 = bf16[256,8192]{1,0:T(8,128)(2,1)} copy(bf16[256,8192]{1,0:T(8,128)(2,1)} %bitcast.8) | data formatting | bytes 8388608
  233.4 0.0 copy-done
  233.4 0.0 copy-start.1
  233.4 2.0 copy.14
  235.4 0.0 copy-done.1
  235.4 0.6 copy.15
  (3 shorter events, 0.0 us)
Async XLA Ops:
  228.6 4.8 %copy-start = (bf16[2,16,8,8192]{3,2,1,0:T(8,128)(2,1)S(1)}, bf16[2,16,8,8192]{3,2,1,0:T(8,128)(2,1)}, u32[]{:S(2)}) copy-start(bf16[2,16,8,8192]{3,2,1,0:T(8,128)(2,1)} %get-tuple-element.7) | copy-start | bytes 12582916
  233.4 2.0 copy-start.1
